TPU v7x, 16 devices: a 4x2x1 block of a 4x4x8 slice. The times are simulated.
16 devices in a mesh: dp: 4 (over y, z, core), tp: 4 (over x).
Axes of the slice: x: 4, y: 2, z: 1, core: 2. Of those that a mesh axis runs over, the one named last changes fastest.
The devices are a block of a 4x4x8 slice.
Arguments:
- x: bfloat16 [8192, 4096], P('dp'), parts along dimension 0
- w_gate: bfloat16 [4096, 12800], P(None, 'tp')
- w_up: bfloat16 [4096, 12800], P(None, 'tp')
- w_down: bfloat16 [12800, 4096], P('tp')
Outputs:
- output: bfloat16 [8192, 4096], P('dp'), parts along dimension 0
There are 4 independent parts. A program takes and returns all parts, laid end to end along the dimension named above; an argument that names none is the same for every part.
All inputs are finite; a program needn't handle non-finite values.
Results may differ from a plain program's by a relative error of at most 0.016.
Values are sent between devices in bfloat16 or wider.
A program may use at most 768 MiB of HBM per device.

v0:
```python
import jax
import jax.numpy as jnp
from jax import lax
from jax.sharding import PartitionSpec as P


def solution(mesh):
    def step(x, w_gate, w_up, w_down):
        gate = jnp.dot(x, w_gate, preferred_element_type=jnp.float32)
        up = jnp.dot(x, w_up, preferred_element_type=jnp.float32)
        hidden = (jax.nn.silu(gate) * up).astype(jnp.bfloat16)
        term = jnp.dot(hidden, w_down, preferred_element_type=jnp.float32).astype(jnp.bfloat16)
        return lax.psum(term, "tp")

    return jax.shard_map(
        step,
        mesh=mesh,
        in_specs=(P("dp", None), P(None, "tp"), P(None, "tp"), P("tp", None)),
        out_specs=P("dp", None),
        check_vma=False,
    )
```

profile of v0, /device:TPU:112, one launch (start us, length us, event | category | flops | bytes accessed | tf_op | source)
XLA Modules:
  0.0 521.7 jit_solution(8055439490909251504)
XLA Ops:
  6.5 0.0 all-reduce.2.cloned.1.call-start
  6.6 69.3 %fusion = f32[2048,3200]{1,0:T(8,128)} fusion(bf16[2048,4096]{1,0:T(8,128)(2,1)} %param.4, bf16[4096,3200]{1,0:T(8,128)(2,1)} %param.5), kind=kOutput, calls=%fused_computation.2 | convolution fusion | flops 53687091200 | bytes 69206016 | tf_op jit(solution)/shard_map/dot_general | solution.py:9
  75.9 72.6 %multiply_convert_fusion = bf16[2048,3200]{1,0:T(8,128)(2,1)S(1)} fusion(f32[2048,3200]{1,0:T(8,128)} %fusion, bf16[2048,4096]{1,0:T(8,128)(2,1)} %param.4, bf16[4096,3200]{1,0:T(8,128)(2,1)} %param.6), kind=kOutput, calls=%fused_computation | convolution fusion | flops 53726412800 | bytes 82313216 | tf_op jit(solution)/shard_map/dot_general | solution.py:10
  148.5 62.2 %convolution_convert_fusion = bf16[2048,4096]{1,0:T(8,128)(2,1)} fusion(bf16[2048,3200]{1,0:T(8,128)(2,1)S(1)} %multiply_convert_fusion, bf16[3200,4096]{1,0:T(8,128)(2,1)} %param.7), kind=kOutput, calls=%fused_computation.1 | convolution fusion | flops 53695479808 | bytes 56098816 | tf_op jit(solution)/shard_map/dot_general | solution.py:12
  210.7 0.1 all-reduce.2.cloned.1.call-update
  210.8 290.0 %all-reduce.2.cloned.1.call-done = bf16[2048,4096]{1,0:T(8,128)(2,1)} async-done(((bf16[2048,4096]{1,0:T(8,128)(2,1)}), bf16[2048,4096]{1,0:T(8,128)(2,1)}) %all-reduce.2.cloned.1.call-update) | async-done | bytes 16777232 | tf_op jit(solution)/shard_map/psum | solution.py:13
  500.8 14.1 %copy.6 = bf16[2048,4096]{1,0:T(8,128)(2,1)} copy(bf16[2048,4096]{1,0:T(8,128)(2,1)} %all-reduce.2.cloned.1.call-done) | data formatting | bytes 33554432
Async XLA Ops:
  6.5 494.2 %all-reduce.2.cloned.1.call-start = ((), (), s32[]{:S(2)}) async-start(), calls=%async_computation | async-start | bytes 33554432 | tf_op jit(solution)/shard_map/psum | solution.py:13
Sparse Core Ops, SparseCore 0:
  210.9 289.8 all-reduce.1
where the time goes:
time: 522 us
  waiting for transfers between devices  290 us (56%)
  matrix products  204 us (39%)
  local copies, waits for them, and re-layouts  14.1 us (3%)
  between operations  13.4 us (3%)
    psum x1, waiting for transfers between devices, step(): return lax.psum(term, 'tp')  290 us
    dot_general x1, matrix products, step(): up = jnp.dot(x, w_up, preferred_element_type=jnp.float32)  72.6 us
    dot_general x1, matrix products, step(): gate = jnp.dot(x, w_gate, preferred_element_type=jnp.float32)  69.3 us
    dot_general x1, matrix products, step(): jnp.dot(hidden, w_down, preferred_element_type=jnp.float32)  62.2 us
    unnamed x1, local copies, waits for them, and re-layouts  14.1 us
  transfers between devices with their start and end apart: 1, of which 1 were waited for; matrix products, arithmetic and copies ran while one was open for 0% of the time, Pallas kernels for 0%

commit v1 on v0

v1 whole, which is shorter than its diff:
```python
import functools

import jax
import jax.numpy as jnp
from jax import lax
from jax.experimental import pallas as pl
from jax.experimental.pallas import tpu as pltpu
from jax.sharding import PartitionSpec as P

MESH = pl.DeviceIdType.MESH
F32, BF16 = jnp.float32, jnp.bfloat16

ROWS = 256
TILE = 640
FWD_AT, OWN_AT = 1, 3
FAR, NEAR, FWD = 0, 1, 2
FIRST, SECOND, PASS = 0, 1, 2


def kernel(
    n, x_hbm, wg_hbm, wu_hbm, wd_hbm, y_hbm,
    xbuf, wbuf, dbuf, hbuf, sbuf, obuf, rbuf,
    x_sem, w_sem, d_sem, y_sem, rs_send, rs_recv, ag_send, ag_recv,
):
    rows, d_model = x_hbm.shape
    ff = wg_hbm.shape[1]
    chunks, tiles = rows // ROWS, ff // TILE
    width = d_model // n
    half = width // 2
    me = lax.axis_index("tp")
    side = (lax.rem(me + n - 1, n), lax.rem(me + 1, n))
    far = lax.rem(me + 2, n)

    def rows_of(c):
        return pl.ds(pl.multiple_of(c * ROWS, ROWS), ROWS)

    def cols_of(shard, h):
        return pl.ds(pl.multiple_of(shard * width + h * half, half), half)

    def x_copy(c):
        slot = lax.rem(c, 2)
        return pltpu.make_async_copy(x_hbm.at[rows_of(c), :], xbuf.at[slot], x_sem.at[slot])

    def w_copies(t):
        slot, j = lax.rem(t, 2), lax.rem(t, tiles)
        cols = pl.ds(pl.multiple_of(j * TILE, TILE), TILE)
        return (
            pltpu.make_async_copy(wg_hbm.at[:, cols], wbuf.at[slot, :, pl.ds(0, TILE)], w_sem.at[slot, 0]),
            pltpu.make_async_copy(wu_hbm.at[:, cols], wbuf.at[slot, :, pl.ds(TILE, TILE)], w_sem.at[slot, 1]),
        )

    pieces = (
        (far, 0), (far, 1), (side[0], 1), (side[1], 0),
        (side[0], 0), (side[1], 1), (me, 0), (me, 1),
    )

    def d_copy(q):
        slot = q % 2
        return pltpu.make_async_copy(wd_hbm.at[:, cols_of(*pieces[q])], dbuf.at[slot], d_sem.at[slot])

    def rs_copy(c, k, a):
        slot = lax.rem(c, 2)
        return pltpu.make_async_remote_copy(
            src_ref=sbuf.at[slot, 2 * k + a],
            dst_ref=rbuf.at[c, 2 * k + a],
            send_sem=rs_send.at[slot, 2 * k + a],
            recv_sem=rs_recv.at[c, 2 * k + a],
            device_id={"tp": side[a]},
            device_id_type=MESH,
        )

    def ag_copy(c, k, a):
        slot = lax.rem(c, 2)
        if k == PASS:
            where = y_hbm.at[rows_of(c), cols_of(side[1 - a], a)]
            src = where
        else:
            h = a if k == FIRST else 1 - a
            where = y_hbm.at[rows_of(c), cols_of(me, h)]
            src = obuf.at[slot, h]
        return pltpu.make_async_remote_copy(
            src_ref=src,
            dst_ref=where,
            send_sem=ag_send.at[slot, 2 * k + a],
            recv_sem=ag_recv.at[c, 2 * k + a],
            device_id={"tp": side[a]},
            device_id_type=MESH,
        )

    def y_copy(c, h):
        slot = lax.rem(c, 2)
        return pltpu.make_async_copy(
            obuf.at[slot, h], y_hbm.at[rows_of(c), cols_of(me, h)], y_sem.at[slot, h]
        )

    def term(c, q):
        if q < 7:
            d_copy(q + 1).start()
        else:
            @pl.when(c + 1 < chunks)
            def _():
                d_copy(0).start()
        d_copy(q).wait()
        return jnp.dot(hbuf[lax.rem(c, 2)], dbuf[q % 2], preferred_element_type=F32)

    def hidden(c, j):
        t = c * tiles + j

        @pl.when(t + 1 < chunks * tiles)
        def _():
            for copy in w_copies(t + 1):
                copy.start()

        @pl.when(j == 0)
        def _():
            @pl.when(c + 1 < chunks)
            def _():
                x_copy(c + 1).start()
            x_copy(c).wait()

        for copy in w_copies(t):
            copy.wait()
        both = jnp.dot(xbuf[lax.rem(c, 2)], wbuf[lax.rem(t, 2)], preferred_element_type=F32)
        gate, up = both[:, :TILE], both[:, TILE:]
        cols = pl.ds(pl.multiple_of(j * TILE, TILE), TILE)
        hbuf[lax.rem(c, 2), :, cols] = (jax.nn.silu(gate) * up).astype(BF16)

    def send_term(c, k, a, acc):
        @pl.when(c >= 2)
        def _():
            rs_copy(c - 2, k, a).wait_send()
        sbuf[lax.rem(c, 2), 2 * k + a] = acc.astype(BF16)
        rs_copy(c, k, a).start()

    def leaves(c):
        for q in range(4):
            k, a = q // 2, q % 2
            send_term(c, k, a, term(c, q))

    def forwards(c):
        for a in range(2):
            rs_copy(c, FAR, a).wait_recv()
            send_term(c, FWD, a, term(c, 4 + a) + rbuf[c, 2 * FAR + a].astype(F32))

    def own(c):
        for h in range(2):
            rs_copy(c, NEAR, 1 - h).wait_recv()
            rs_copy(c, FWD, h).wait_recv()
            acc = term(c, 6 + h) + rbuf[c, 2 * NEAR + 1 - h].astype(F32) + rbuf[c, 2 * FWD + h].astype(F32)

            @pl.when(c >= 2)
            def _():
                y_copy(c - 2, h).wait()
                ag_copy(c - 2, FIRST, h).wait_send()
                ag_copy(c - 2, SECOND, 1 - h).wait_send()
            obuf[lax.rem(c, 2), h] = acc.astype(BF16)
            y_copy(c, h).start()
            ag_copy(c, FIRST, h).start()
        for a in range(2):
            ag_copy(c, SECOND, a).start()

    def passes(c):
        for a in range(2):
            @pl.when(c >= 2)
            def _():
                ag_copy(c - 2, PASS, a).wait_send()
            ag_copy(c, FIRST, a).wait_recv()
            ag_copy(c, PASS, a).start()

    x_copy(0).start()
    for copy in w_copies(0):
        copy.start()
    d_copy(0).start()

    barrier = pltpu.get_barrier_semaphore()
    for a in range(2):
        pl.semaphore_signal(barrier, inc=1, device_id={"tp": side[a]}, device_id_type=MESH)
    pl.semaphore_wait(barrier, 2)

    @pl.loop(0, chunks + 1)
    def _(c):
        @pl.loop(0, tiles)
        def _(j):
            @pl.when(c < chunks)
            def _():
                hidden(c, j)

            @pl.when(jnp.logical_and(c >= 1, j == FWD_AT))
            def _():
                forwards(c - 1)

            @pl.when(jnp.logical_and(c >= 1, j == OWN_AT))
            def _():
                own(c - 1)

        @pl.when(c < chunks)
        def _():
            leaves(c)

        @pl.when(c >= 1)
        def _():
            passes(c - 1)

    @pl.loop(chunks - 2, chunks)
    def _(c):
        for a in range(2):
            for k in range(3):
                rs_copy(c, k, a).wait_send()
                ag_copy(c, k, a).wait_send()
            y_copy(c, a).wait()

    @pl.loop(0, chunks)
    def _(c):
        for a in range(2):
            ag_copy(c, SECOND, a).wait_recv()
            ag_copy(c, PASS, a).wait_recv()


def solution(mesh):
    n = mesh.shape["tp"]

    def step(x, w_gate, w_up, w_down):
        rows, d_model = x.shape
        ff = w_gate.shape[1]
        chunks, half = rows // ROWS, d_model // n // 2
        assert n == 4 and rows % ROWS == 0 and ff % TILE == 0
        dma = pltpu.SemaphoreType.DMA
        flops = 6 * rows * d_model * ff
        return pl.pallas_call(
            functools.partial(kernel, n),
            out_shape=jax.ShapeDtypeStruct((rows, d_model), BF16),
            in_specs=[pl.BlockSpec(memory_space=pl.ANY)] * 4,
            out_specs=pl.BlockSpec(memory_space=pl.ANY),
            scratch_shapes=[
                pltpu.VMEM((2, ROWS, d_model), BF16),
                pltpu.VMEM((2, d_model, 2 * TILE), BF16),
                pltpu.VMEM((2, ff, half), BF16),
                pltpu.VMEM((2, ROWS, ff), BF16),
                pltpu.VMEM((2, 6, ROWS, half), BF16),
                pltpu.VMEM((2, 2, ROWS, half), BF16),
                pltpu.VMEM((chunks, 6, ROWS, half), BF16),
                dma((2,)), dma((2, 2)), dma((2,)), dma((2, 2)),
                dma((2, 6)), dma((chunks, 6)), dma((2, 6)), dma((chunks, 6)),
            ],
            compiler_params=pltpu.CompilerParams(
                collective_id=0, has_side_effects=True, vmem_limit_bytes=62 * 1024 * 1024
            ),
            cost_estimate=pl.CostEstimate(
                flops=flops, bytes_accessed=chunks * 6 * d_model * ff, transcendentals=rows * ff
            ),
        )(x, w_gate, w_up, w_down)

    return jax.shard_map(
        step,
        mesh=mesh,
        in_specs=(P("dp", None), P(None, "tp"), P(None, "tp"), P("tp", None)),
        out_specs=P("dp", None),
        check_vma=False,
    )
```

time: 522 us -> 329 us (0.63)
  Pallas kernels: 0 us -> 314 us
  waiting for transfers between devices: 290 us -> 0 us
  matrix products: 204 us -> 0 us
  between operations: 13.4 us -> 0.01 us
    pallas_call x0 -> x1, Pallas kernels: none -> 314 us  [step(): pl.pallas_call(functools.partial(kernel, n), out_shape=jax.ShapeDtypeStru...]
    psum x1 -> x0, waiting for transfers between devices: 290 us -> none  [step(): return lax.psum(term, 'tp')]
    dot_general x3 -> x0, matrix products: 204 us -> none  [the longest x1 72.6 us: step(): up = jnp.dot(x, w_up, preferred_element_type=jnp.float32)]
  transfers between devices with their start and end apart: 1 -> 0, of which waited for: 1 -> 0; matrix products, arithmetic and copies ran while one was open for 0% -> 0% of each run, Pallas kernels for 0% -> 0%
where the time goes in v1:
time: 329 us; the launch traced here: 328 us
  Pallas kernels  314 us (95%)
  local copies, waits for them, and re-layouts  14.1 us (4%)
    pallas_call x1, Pallas kernels, step(): pl.pallas_call(functools.partial(kernel, n), out_shape=jax.ShapeDtypeStru...  314 us
    unnamed x1, local copies, waits for them, and re-layouts  14.1 us

profile of v1, /device:TPU:112, one launch (start us, length us, event | category | flops | bytes accessed | tf_op | source)
XLA Modules:
  0.0 328.0 jit_solution(1661458558427848524)
XLA Ops:
  0.0 313.9 %shard_map.46 = bf16[2048,4096]{1,0:T(8,128)(2,1)} custom-call(bf16[2048,4096]{1,0:T(8,128)(2,1)} %x_hbm.1, bf16[4096,3200]{1,0:T(8,128)(2,1)} %wg_hbm.1, bf16[4096,3200]{1,0:T(8,128)(2,1)} %wu_hbm.1, bf16[3200,4096]{1,0:T(8,128)(2,1)} %wd_hbm.1), custom_call_target="tpu_custom_call" | custom-call | flops 161061273600 | bytes 629145600 | tf_op jit(solution)/shard_map/pallas_call | solution.py:229
  313.9 14.1 %copy.6 = bf16[2048,4096]{1,0:T(8,128)(2,1)} copy(bf16[2048,4096]{1,0:T(8,128)(2,1)} %shard_map.46) | data formatting | bytes 33554432

commit v2 on v1

--- a/solution.py
+++ b/solution.py
@@ -12,15 +12,15 @@
 
 ROWS = 256
 TILE = 640
-FWD_AT, OWN_AT = 1, 3
+FWD_AT, OWN_AT = 0, 2
 FAR, NEAR, FWD = 0, 1, 2
 FIRST, SECOND, PASS = 0, 1, 2
 
 
 def kernel(
-    n, x_hbm, wg_hbm, wu_hbm, wd_hbm, y_hbm,
-    xbuf, wbuf, dbuf, hbuf, sbuf, obuf, rbuf,
-    x_sem, w_sem, d_sem, y_sem, rs_send, rs_recv, ag_send, ag_recv,
+    n, x_hbm, wg_hbm, wu_hbm, wd_hbm, y_ref,
+    xbuf, wbuf, dbuf, hbuf, sbuf, nbuf,
+    x_sem, w_sem, d_sem, rs_send, rs_recv, ag_send, ag_recv,
 ):
     rows, d_model = x_hbm.shape
     ff = wg_hbm.shape[1]
@@ -58,40 +58,31 @@
         slot = q % 2
         return pltpu.make_async_copy(wd_hbm.at[:, cols_of(*pieces[q])], dbuf.at[slot], d_sem.at[slot])
 
+    def place(c, shard, h):
+        return y_ref.at[rows_of(c), cols_of(shard, h)]
+
+    def send(src, dst, send_sem, recv_sem, a):
+        return pltpu.make_async_remote_copy(
+            src_ref=src, dst_ref=dst, send_sem=send_sem, recv_sem=recv_sem,
+            device_id={"tp": side[a]}, device_id_type=MESH,
+        )
+
     def rs_copy(c, k, a):
-        slot = lax.rem(c, 2)
-        return pltpu.make_async_remote_copy(
-            src_ref=sbuf.at[slot, 2 * k + a],
-            dst_ref=rbuf.at[c, 2 * k + a],
-            send_sem=rs_send.at[slot, 2 * k + a],
-            recv_sem=rs_recv.at[c, 2 * k + a],
-            device_id={"tp": side[a]},
-            device_id_type=MESH,
-        )
+        slot, i = lax.rem(c, 2), 2 * k + a
+        if k == FAR:
+            dst = place(c, far, a)
+        elif k == NEAR:
+            dst = nbuf.at[c, a]
+        else:
+            dst = place(c, side[a], a)
+        return send(sbuf.at[slot, i], dst, rs_send.at[slot, i], rs_recv.at[c, i], a)
 
     def ag_copy(c, k, a):
-        slot = lax.rem(c, 2)
         if k == PASS:
-            where = y_hbm.at[rows_of(c), cols_of(side[1 - a], a)]
-            src = where
+            where = place(c, side[1 - a], a)
         else:
-            h = a if k == FIRST else 1 - a
-            where = y_hbm.at[rows_of(c), cols_of(me, h)]
-            src = obuf.at[slot, h]
-        return pltpu.make_async_remote_copy(
-            src_ref=src,
-            dst_ref=where,
-            send_sem=ag_send.at[slot, 2 * k + a],
-            recv_sem=ag_recv.at[c, 2 * k + a],
-            device_id={"tp": side[a]},
-            device_id_type=MESH,
-        )
-
-    def y_copy(c, h):
-        slot = lax.rem(c, 2)
-        return pltpu.make_async_copy(
-            obuf.at[slot, h], y_hbm.at[rows_of(c), cols_of(me, h)], y_sem.at[slot, h]
-        )
+            where = place(c, me, a if k == FIRST else 1 - a)
+        return send(where, where, ag_send.at[lax.rem(c, 2), 2 * k + a], ag_recv.at[c, 2 * k + a], a)
 
     def term(c, q):
         if q < 7:
@@ -125,45 +116,42 @@
         cols = pl.ds(pl.multiple_of(j * TILE, TILE), TILE)
         hbuf[lax.rem(c, 2), :, cols] = (jax.nn.silu(gate) * up).astype(BF16)
 
-    def send_term(c, k, a, acc):
+    def free(c, copies):
         @pl.when(c >= 2)
         def _():
-            rs_copy(c - 2, k, a).wait_send()
-        sbuf[lax.rem(c, 2), 2 * k + a] = acc.astype(BF16)
-        rs_copy(c, k, a).start()
+            for copy, k, a in copies:
+                copy(c - 2, k, a).wait_send()
 
     def leaves(c):
         for q in range(4):
             k, a = q // 2, q % 2
-            send_term(c, k, a, term(c, q))
+            free(c, [(rs_copy, k, a)])
+            sbuf[lax.rem(c, 2), 2 * k + a] = term(c, q).astype(BF16)
+            rs_copy(c, k, a).start()
 
     def forwards(c):
         for a in range(2):
+            free(c, [(rs_copy, FWD, a)])
             rs_copy(c, FAR, a).wait_recv()
-            send_term(c, FWD, a, term(c, 4 + a) + rbuf[c, 2 * FAR + a].astype(F32))
+            total = term(c, 4 + a) + y_ref[rows_of(c), cols_of(side[a], a)].astype(F32)
+            sbuf[lax.rem(c, 2), 2 * FWD + a] = total.astype(BF16)
+            rs_copy(c, FWD, a).start()
 
     def own(c):
         for h in range(2):
+            free(c, [(ag_copy, FIRST, h), (ag_copy, SECOND, 1 - h)])
+            at = (rows_of(c), cols_of(me, h))
             rs_copy(c, NEAR, 1 - h).wait_recv()
             rs_copy(c, FWD, h).wait_recv()
-            acc = term(c, 6 + h) + rbuf[c, 2 * NEAR + 1 - h].astype(F32) + rbuf[c, 2 * FWD + h].astype(F32)
-
-            @pl.when(c >= 2)
-            def _():
-                y_copy(c - 2, h).wait()
-                ag_copy(c - 2, FIRST, h).wait_send()
-                ag_copy(c - 2, SECOND, 1 - h).wait_send()
-            obuf[lax.rem(c, 2), h] = acc.astype(BF16)
-            y_copy(c, h).start()
+            total = term(c, 6 + h) + nbuf[c, 1 - h].astype(F32) + y_ref[at].astype(F32)
+            y_ref[at] = total.astype(BF16)
             ag_copy(c, FIRST, h).start()
         for a in range(2):
             ag_copy(c, SECOND, a).start()
 
     def passes(c):
         for a in range(2):
-            @pl.when(c >= 2)
-            def _():
-                ag_copy(c - 2, PASS, a).wait_send()
+            free(c, [(ag_copy, PASS, a)])
             ag_copy(c, FIRST, a).wait_recv()
             ag_copy(c, PASS, a).start()
 
@@ -189,6 +177,10 @@
             def _():
                 forwards(c - 1)
 
+            @pl.when(jnp.logical_and(c >= 2, j == FWD_AT))
+            def _():
+                passes(c - 2)
+
             @pl.when(jnp.logical_and(c >= 1, j == OWN_AT))
             def _():
                 own(c - 1)
@@ -197,9 +189,7 @@
         def _():
             leaves(c)
 
-        @pl.when(c >= 1)
-        def _():
-            passes(c - 1)
+    passes(chunks - 1)
 
     @pl.loop(chunks - 2, chunks)
     def _(c):
@@ -207,7 +197,6 @@
             for k in range(3):
                 rs_copy(c, k, a).wait_send()
                 ag_copy(c, k, a).wait_send()
-            y_copy(c, a).wait()
 
     @pl.loop(0, chunks)
     def _(c):
@@ -228,22 +217,21 @@
         flops = 6 * rows * d_model * ff
         return pl.pallas_call(
             functools.partial(kernel, n),
-            out_shape=jax.ShapeDtypeStruct((rows, d_model), BF16),
+            out_shape=pltpu.VMEM((rows, d_model), BF16),
             in_specs=[pl.BlockSpec(memory_space=pl.ANY)] * 4,
-            out_specs=pl.BlockSpec(memory_space=pl.ANY),
+            out_specs=pl.BlockSpec(memory_space=pltpu.VMEM),
             scratch_shapes=[
                 pltpu.VMEM((2, ROWS, d_model), BF16),
                 pltpu.VMEM((2, d_model, 2 * TILE), BF16),
                 pltpu.VMEM((2, ff, half), BF16),
                 pltpu.VMEM((2, ROWS, ff), BF16),
                 pltpu.VMEM((2, 6, ROWS, half), BF16),
-                pltpu.VMEM((2, 2, ROWS, half), BF16),
-                pltpu.VMEM((chunks, 6, ROWS, half), BF16),
-                dma((2,)), dma((2, 2)), dma((2,)), dma((2, 2)),
+                pltpu.VMEM((chunks, 2, ROWS, half), BF16),
+                dma((2,)), dma((2, 2)), dma((2,)),
                 dma((2, 6)), dma((chunks, 6)), dma((2, 6)), dma((chunks, 6)),
             ],
             compiler_params=pltpu.CompilerParams(
-                collective_id=0, has_side_effects=True, vmem_limit_bytes=62 * 1024 * 1024
+                collective_id=0, has_side_effects=True, vmem_limit_bytes=45 * 1024 * 1024
             ),
             cost_estimate=pl.CostEstimate(
                 flops=flops, bytes_accessed=chunks * 6 * d_model * ff, transcendentals=rows * ff

time: 329 us -> 311 us (0.945)
  Pallas kernels: 314 us -> 304 us
  local copies, waits for them, and re-layouts: 14.1 us -> 6.16 us
    pallas_call x1, Pallas kernels: 314 us -> 304 us  [step(): pl.pallas_call(functools.partial(kernel, n), out_shape=pltpu.VMEM((rows,...]
    unnamed x1, local copies, waits for them, and re-layouts: 14.1 us -> 6.16 us
where the time goes in v2:
time: 311 us; the launch traced here: 310 us
  Pallas kernels  304 us (98%)
  local copies, waits for them, and re-layouts  6.16 us (2%)
    pallas_call x1, Pallas kernels, step(): pl.pallas_call(functools.partial(kernel, n), out_shape=pltpu.VMEM((rows,...  304 us

profile of v2, /device:TPU:112, one launch (start us, length us, event | category | flops | bytes accessed | tf_op | source)
XLA Modules:
  0.0 310.2 jit_solution(8146451002478813834)
XLA Ops:
  0.0 304.1 %shard_map.46 = bf16[2048,4096]{1,0:T(8,128)(2,1)S(1)} custom-call(bf16[2048,4096]{1,0:T(8,128)(2,1)} %x_hbm.1, bf16[4096,3200]{1,0:T(8,128)(2,1)} %wg_hbm.1, bf16[4096,3200]{1,0:T(8,128)(2,1)} %wu_hbm.1, bf16[3200,4096]{1,0:T(8,128)(2,1)} %wd_hbm.1), custom_call_target="tpu_custom_call" | custom-call | flops 161061273600 | bytes 629145600 | tf_op jit(solution)/shard_map/pallas_call | solution.py:218
  304.1 6.2 %copy.6 = bf16[2048,4096]{1,0:T(8,128)(2,1)} copy(bf16[2048,4096]{1,0:T(8,128)(2,1)S(1)} %shard_map.46) | data formatting | bytes 33554432

commit v3 on v2

v3 whole, which is shorter than its diff:
```python
import functools

import jax
import jax.numpy as jnp
from jax import lax
from jax.experimental import pallas as pl
from jax.experimental.pallas import tpu as pltpu
from jax.sharding import PartitionSpec as P

MESH = pl.DeviceIdType.MESH
F32, BF16 = jnp.float32, jnp.bfloat16

ROWS = 256
TILE = 640
PARTS = 2
AHEAD = 3
D_SLOTS = 2
SUB = 2
FWD_AT, OWN_AT = 0, 2
FAR, NEAR, FWD = 0, 1, 2
FIRST, SECOND, PASS = 0, 1, 2


def kernel(
    n, x_hbm, wg_hbm, wu_hbm, wd_hbm, y_ref,
    xbuf, wbuf, dbuf, hbuf, sbuf, nbuf,
    x_sem, w_sem, d_sem, rs_send, rs_recv, ag_send, ag_recv,
):
    rows, d_model = x_hbm.shape
    ff = wg_hbm.shape[1]
    chunks, tiles = rows // ROWS, ff // TILE
    width = d_model // n
    half = width // 2
    depth = d_model // PARTS
    sub = ROWS // SUB
    me = lax.axis_index("tp")
    side = (lax.rem(me + n - 1, n), lax.rem(me + 1, n))
    far = lax.rem(me + 2, n)

    def rows_of(c, r=None):
        if r is None:
            return pl.ds(pl.multiple_of(c * ROWS, ROWS), ROWS)
        return pl.ds(pl.multiple_of(c * ROWS + r * sub, sub), sub)

    def cols_of(shard, h):
        return pl.ds(pl.multiple_of(shard * width + h * half, half), half)

    def x_copy(c):
        slot = lax.rem(c, 2)
        return pltpu.make_async_copy(x_hbm.at[rows_of(c), :], xbuf.at[slot], x_sem.at[slot])

    def w_copies(t):
        slot = lax.rem(t, AHEAD + 1)
        deep = pl.ds(pl.multiple_of(lax.rem(t, PARTS) * depth, depth), depth)
        cols = pl.ds(pl.multiple_of(lax.rem(t // PARTS, tiles) * TILE, TILE), TILE)
        return (
            pltpu.make_async_copy(wg_hbm.at[deep, cols], wbuf.at[slot, :, pl.ds(0, TILE)], w_sem.at[slot, 0]),
            pltpu.make_async_copy(wu_hbm.at[deep, cols], wbuf.at[slot, :, pl.ds(TILE, TILE)], w_sem.at[slot, 1]),
        )

    pieces = (
        (far, 0), (far, 1), (side[0], 1), (side[1], 0),
        (side[0], 0), (side[1], 1), (me, 0), (me, 1),
    )

    def d_copy(q):
        slot = q % D_SLOTS
        return pltpu.make_async_copy(wd_hbm.at[:, cols_of(*pieces[q])], dbuf.at[slot], d_sem.at[slot])

    def place(c, shard, h):
        return y_ref.at[rows_of(c), cols_of(shard, h)]

    def send(src, dst, send_sem, recv_sem, a):
        return pltpu.make_async_remote_copy(
            src_ref=src, dst_ref=dst, send_sem=send_sem, recv_sem=recv_sem,
            device_id={"tp": side[a]}, device_id_type=MESH,
        )

    def rs_copy(c, k, a, r=0):
        slot, i = lax.rem(c, 2), 2 * k + a
        src = sbuf.at[slot, i]
        if k == FAR:
            dst = place(c, far, a)
        elif k == NEAR:
            dst = nbuf.at[slot, a]
        else:
            src = sbuf.at[slot, i, pl.ds(r * sub, sub)]
            dst = y_ref.at[rows_of(c, r), cols_of(side[a], a)]
            i += 2 * r
        return send(src, dst, rs_send.at[slot, i], rs_recv.at[c, i], a)

    def ag_copy(c, k, a, r=0):
        if k == PASS:
            where = place(c, side[1 - a], a)
        elif k == SECOND:
            where = place(c, me, 1 - a)
        else:
            where = y_ref.at[rows_of(c, r), cols_of(me, a)]
        i = a + 2 * (r if k == FIRST else SUB - 1 + k)
        return send(where, where, ag_send.at[lax.rem(c, 2), i], ag_recv.at[c, i], a)

    def term(c, q, rows=slice(None)):
        return jnp.dot(hbuf[lax.rem(c, 2), rows], dbuf[q % D_SLOTS], preferred_element_type=F32)

    def refill(c, q):
        if q + D_SLOTS < len(pieces):
            d_copy(q + D_SLOTS).start()
        else:
            @pl.when(c + 1 < chunks)
            def _():
                d_copy(q + D_SLOTS - len(pieces)).start()

    def hidden(c, j):
        @pl.when(j == 0)
        def _():
            @pl.when(c + 1 < chunks)
            def _():
                x_copy(c + 1).start()
            x_copy(c).wait()

        both = None
        for p in range(PARTS):
            t = (c * tiles + j) * PARTS + p

            @pl.when(t + AHEAD < chunks * tiles * PARTS)
            def _():
                for copy in w_copies(t + AHEAD):
                    copy.start()

            for copy in w_copies(t):
                copy.wait()
            part = jnp.dot(
                xbuf[lax.rem(c, 2), :, p * depth : (p + 1) * depth],
                wbuf[lax.rem(t, AHEAD + 1)],
                preferred_element_type=F32,
            )
            both = part if p == 0 else both + part
        gate, up = both[:, :TILE], both[:, TILE:]
        cols = pl.ds(pl.multiple_of(j * TILE, TILE), TILE)
        hbuf[lax.rem(c, 2), :, cols] = (jax.nn.silu(gate) * up).astype(BF16)

    def free(c, *copies):
        @pl.when(c >= 2)
        def _():
            for copy, *which in copies:
                copy(c - 2, *which).wait_send()

    def leaves(c):
        for q in range(4):
            k, a = q // 2, q % 2
            free(c, (rs_copy, k, a))
            d_copy(q).wait()
            sbuf[lax.rem(c, 2), 2 * k + a] = term(c, q).astype(BF16)
            rs_copy(c, k, a).start()
            refill(c, q)

    def forwards(c):
        for r in range(SUB):
            part = slice(r * sub, (r + 1) * sub)
            for a in range(2):
                free(c, (rs_copy, FWD, a, r))
                if r == 0:
                    d_copy(4 + a).wait()
                    rs_copy(c, FAR, a).wait_recv()
                arrived = y_ref[rows_of(c, r), cols_of(side[a], a)].astype(F32)
                total = term(c, 4 + a, part) + arrived
                sbuf[lax.rem(c, 2), 2 * FWD + a, part] = total.astype(BF16)
                rs_copy(c, FWD, a, r).start()
                if r == SUB - 1:
                    refill(c, 4 + a)

    def own(c):
        for r in range(SUB):
            part = slice(r * sub, (r + 1) * sub)
            for h in range(2):
                free(c, (ag_copy, FIRST, h, r))
                if r == 0:
                    d_copy(6 + h).wait()
                    rs_copy(c, NEAR, 1 - h).wait_recv()
                rs_copy(c, FWD, h, r).wait_recv()
                at = (rows_of(c, r), cols_of(me, h))
                direct = nbuf[lax.rem(c, 2), 1 - h, part].astype(F32)
                y_ref[at] = (term(c, 6 + h, part) + direct + y_ref[at].astype(F32)).astype(BF16)
                ag_copy(c, FIRST, h, r).start()
                if r == SUB - 1:
                    refill(c, 6 + h)
        for a in range(2):
            free(c, (ag_copy, SECOND, a))
            ag_copy(c, SECOND, a).start()

    def passes(c):
        for a in range(2):
            free(c, (ag_copy, PASS, a))
            for r in range(SUB):
                ag_copy(c, FIRST, a, r).wait_recv()
            ag_copy(c, PASS, a).start()

    x_copy(0).start()
    for t in range(AHEAD):
        for copy in w_copies(t):
            copy.start()
    for q in range(D_SLOTS):
        d_copy(q).start()

    barrier = pltpu.get_barrier_semaphore()
    for a in range(2):
        pl.semaphore_signal(barrier, inc=1, device_id={"tp": side[a]}, device_id_type=MESH)
    pl.semaphore_wait(barrier, 2)

    @pl.loop(0, chunks + 1)
    def _(c):
        @pl.loop(0, tiles)
        def _(j):
            @pl.when(c < chunks)
            def _():
                hidden(c, j)

            @pl.when(jnp.logical_and(c >= 1, j == FWD_AT))
            def _():
                forwards(c - 1)

            @pl.when(jnp.logical_and(c >= 2, j == FWD_AT))
            def _():
                passes(c - 2)

            @pl.when(jnp.logical_and(c >= 1, j == OWN_AT))
            def _():
                own(c - 1)

        @pl.when(c < chunks)
        def _():
            leaves(c)

    passes(chunks - 1)

    @pl.loop(chunks - 2, chunks)
    def _(c):
        for a in range(2):
            for k in (FAR, NEAR):
                rs_copy(c, k, a).wait_send()
            for k in (SECOND, PASS):
                ag_copy(c, k, a).wait_send()
            for r in range(SUB):
                rs_copy(c, FWD, a, r).wait_send()
                ag_copy(c, FIRST, a, r).wait_send()

    @pl.loop(0, chunks)
    def _(c):
        for a in range(2):
            ag_copy(c, SECOND, a).wait_recv()
            ag_copy(c, PASS, a).wait_recv()


def solution(mesh):
    n = mesh.shape["tp"]

    def step(x, w_gate, w_up, w_down):
        rows, d_model = x.shape
        ff = w_gate.shape[1]
        chunks, half = rows // ROWS, d_model // n // 2
        assert n == 4 and rows % ROWS == 0 and ff % TILE == 0
        dma, kinds = pltpu.SemaphoreType.DMA, 4 + 2 * SUB
        flops = 6 * rows * d_model * ff
        return pl.pallas_call(
            functools.partial(kernel, n),
            out_shape=pltpu.VMEM((rows, d_model), BF16),
            in_specs=[pl.BlockSpec(memory_space=pl.ANY)] * 4,
            out_specs=pl.BlockSpec(memory_space=pltpu.VMEM),
            scratch_shapes=[
                pltpu.VMEM((2, ROWS, d_model), BF16),
                pltpu.VMEM((AHEAD + 1, d_model // PARTS, 2 * TILE), BF16),
                pltpu.VMEM((D_SLOTS, ff, half), BF16),
                pltpu.VMEM((2, ROWS, ff), BF16),
                pltpu.VMEM((2, 6, ROWS, half), BF16),
                pltpu.VMEM((2, 2, ROWS, half), BF16),
                dma((2,)), dma((AHEAD + 1, 2)), dma((D_SLOTS,)),
                dma((2, kinds)), dma((chunks, kinds)), dma((2, kinds)), dma((chunks, kinds)),
            ],
            compiler_params=pltpu.CompilerParams(
                collective_id=0, has_side_effects=True, vmem_limit_bytes=45 * 1024 * 1024
            ),
            cost_estimate=pl.CostEstimate(
                flops=flops, bytes_accessed=chunks * 6 * d_model * ff, transcendentals=rows * ff
            ),
        )(x, w_gate, w_up, w_down)

    return jax.shard_map(
        step,
        mesh=mesh,
        in_specs=(P("dp", None), P(None, "tp"), P(None, "tp"), P("tp", None)),
        out_specs=P("dp", None),
        check_vma=False,
    )
```

time: 311 us -> 308 us (level)
  no operation moved by 1% of the time
where the time goes in v3:
time: 308 us
  Pallas kernels  302 us (98%)
  local copies, waits for them, and re-layouts  6.16 us (2%)
    pallas_call x1, Pallas kernels, step(): pl.pallas_call(functools.partial(kernel, n), out_shape=pltpu.VMEM((rows,...  302 us
    unnamed x1, local copies, waits for them, and re-layouts  6.16 us

profile of v3, /device:TPU:112, one launch (start us, length us, event | category | flops | bytes accessed | tf_op | source)
XLA Modules:
  0.0 307.8 jit_solution(6889780322102222210)
XLA Ops:
  0.0 301.6 %shard_map.46 = bf16[2048,4096]{1,0:T(8,128)(2,1)S(1)} custom-call(bf16[2048,4096]{1,0:T(8,128)(2,1)} %x_hbm.1, bf16[4096,3200]{1,0:T(8,128)(2,1)} %wg_hbm.1, bf16[4096,3200]{1,0:T(8,128)(2,1)} %wu_hbm.1, bf16[3200,4096]{1,0:T(8,128)(2,1)} %wd_hbm.1), custom_call_target="tpu_custom_call" | custom-call | flops 161061273600 | bytes 629145600 | tf_op jit(solution)/shard_map/pallas_call | solution.py:264
  301.7 6.2 %copy.6 = bf16[2048,4096]{1,0:T(8,128)(2,1)} copy(bf16[2048,4096]{1,0:T(8,128)(2,1)S(1)} %shard_map.46) | data formatting | bytes 33554432
